TPU v7x, 256 devices: a whole 4x4x8 slice. The times are simulated.
256 devices in a mesh: gx: 8 (over x, core), gy: 4 (over z_hi), gz: 8 (over z_lo, y).
Axes of the slice: x: 4, y: 4, z: 8 (z_hi: 4, z_lo: 2; z = z_hi * 2 + z_lo), core: 2. Of those that a mesh axis runs over, the one named last changes fastest.
Arguments:
- hidden_rows: bfloat16 [4096, 16384], P(('gx', 'gy'), 'gz'), may hold values from -2000 to 2000
- norm_gain: bfloat16 [16384], P('gz'), may hold values from 0.5 to 1.5
- w_query: bfloat16 [16384, 16384], P('gz', ('gx', 'gy')), may hold values from -0.046875 to 0.046875
- w_keyval: bfloat16 [16384, 2048], P('gz', ('gx', 'gy')), may hold values from -0.046875 to 0.046875
- positions: int32 [4096], P('gz'), may hold values from 0 to 1023, as said below
- keyval_order: int32 [8], replicated, may hold values from 0 to 7, each once
Outputs:
- queries: bfloat16 [4096, 16384], P('gz', ('gx', 'gy'))
- keyval_owned: bfloat16 [8, 4096, 256], P('gy', 'gz')
Inputs may be any that keep to these rules, and one draw needn't show every extreme that they name: `positions`: each token's position within its packed document: 0 where a document starts, else one more than the previous token's; a document holds at most 1024 tokens. `keyval_order`: each head once.
All inputs are finite; a program needn't handle non-finite values.
Results may differ from a plain program's by a relative error of at most 0.0066.
Values may be sent and summed in bfloat16 or wider, within the bound.
A program may use at most 128 MiB of HBM per device.

v0:
```python
import math
import jax
import jax.numpy as jnp
from jax import lax
from jax.sharding import PartitionSpec as P

D = 16384
KVH = 8
HD = 128
rope_base = 500000.0
norm_eps = 1e-05


def from_everyone(value, axis):
    copies = jnp.broadcast_to(value, (lax.axis_size(axis), *value.shape))
    return lax.all_to_all(copies, axis, split_axis=0, concat_axis=0, tiled=True)


def taken_together(value, axis):
    everything = from_everyone(value, axis)
    return jnp.sum(everything, axis=0)


def in_blocks(value, dim, count):
    before, after = (value.shape[:dim], value.shape[dim + 1 :])
    return jnp.moveaxis(value.reshape(*before, count, -1, *after), dim, 0)


def summed_on_arrival(value, axis, dim):
    count = lax.axis_size(axis)
    blocks = lax.all_to_all(in_blocks(value, dim, count), axis, 0, 0, tiled=True)
    return jnp.sum(blocks.astype(jnp.float32), axis=0)


def rotate_pairs(values, position_ids, col_start, keys_only):
    row_total, col_width = values.shape
    pair_col = col_start + 2 * jnp.arange(col_width // 2, dtype=jnp.int32)
    within = pair_col % HD
    inv_freq = jnp.exp((within // 2).astype(jnp.float32) * (-2.0 * math.log(rope_base) / HD))
    angles = position_ids.astype(jnp.float32)[:, None] * inv_freq[None, :]
    cosines = jnp.cos(angles)
    sine_part = jnp.sin(angles)
    paired = values.reshape(row_total, col_width // 2, 2)
    even_part = paired[..., 0]
    odd_part = paired[..., 1]
    rotated = jnp.stack(
        [even_part * cosines - odd_part * sine_part, even_part * sine_part + odd_part * cosines],
        axis=-1,
    )
    if keys_only:
        is_key = (pair_col // HD % 2 == 0)[None, :, None]
        rotated = jnp.where(is_key, rotated, paired)
    return rotated.reshape(row_total, col_width)


def body(hidden_rows, norm_gain, w_query, w_keyval, positions, keyval_order):
    widened_gain = norm_gain.astype(jnp.float32)
    widened = hidden_rows.astype(jnp.float32)
    factor = lax.rsqrt(taken_together(jnp.sum(widened * widened, axis=1), "gz") / D + norm_eps)
    normed_rows = (
        hidden_rows.astype(jnp.float32) * factor[:, None] * widened_gain[None, :]
    ).astype(jnp.bfloat16)
    query_width = w_query.shape[1]
    keyval_width = w_keyval.shape[1]
    group_size = lax.axis_size("gy")
    gathered = lax.all_gather(normed_rows, ("gx", "gy"), axis=0, tiled=True)
    query_sum = summed_on_arrival(
        jnp.dot(gathered, w_query, preferred_element_type=jnp.float32).astype(jnp.bfloat16), "gz", 0
    )
    keyval_sum = summed_on_arrival(
        jnp.dot(gathered, w_keyval, preferred_element_type=jnp.float32).astype(jnp.bfloat16),
        "gz",
        0,
    )
    col_index = lax.axis_index("gx") * group_size + lax.axis_index("gy")
    queries = rotate_pairs(query_sum, positions, col_index * query_width, False).astype(
        jnp.bfloat16
    )
    keyval_part = rotate_pairs(keyval_sum, positions, col_index * keyval_width, True).astype(
        jnp.bfloat16
    )
    keyval_all = lax.all_gather(keyval_part, ("gx", "gy"), axis=1, tiled=True)
    slot_count = KVH // group_size
    first_slot = lax.axis_index("gy") * slot_count
    keyval_heads = keyval_all.reshape(keyval_all.shape[0], KVH, 2 * HD)
    wanted = lax.dynamic_slice_in_dim(keyval_order, first_slot, slot_count, 0)
    selector = (wanted[:, None] == jnp.arange(KVH, dtype=jnp.int32)[None, :]).astype(jnp.bfloat16)
    keyval_owned = jnp.einsum(
        "sh,rhc->src", selector, keyval_heads, preferred_element_type=jnp.float32
    ).astype(jnp.bfloat16)
    return (queries, keyval_owned)


def solution(mesh):
    in_specs = (
        P(("gx", "gy"), "gz"),
        P("gz"),
        P("gz", ("gx", "gy")),
        P("gz", ("gx", "gy")),
        P("gz"),
        P(),
    )
    out_specs = (P("gz", ("gx", "gy")), P("gy", "gz", None))
    return jax.shard_map(body, mesh=mesh, in_specs=in_specs, out_specs=out_specs, check_vma=False)
```

profile of v0, /device:TPU:1, one launch (start us, length us, event | category | flops | bytes accessed | tf_op | source)
XLA Modules:
  0.0 268.1 jit_solution(16777390107375378753)
XLA Ops:
  7.2 1.4 fusion
  8.6 0.6 broadcast_in_dim.14
  9.2 6.4 %all-to-all-start = ((f32[8,1,128]{2,1,0:T(1,128)}), f32[8,1,128]{2,1,0:T(1,128)S(1)}, u32[]{:S(2)}, u32[]{:S(2)}) async-start(f32[8,1,128]{2,1,0:T(1,128)} %broadcast_in_dim.14), calls=%async_computation | async-start | bytes 8192 | tf_op jit(solution)/shard_map/all_to_all | solution.py:16
  15.6 0.7 convert_element_type.52
  16.3 4.2 %all-to-all-done = f32[8,1,128]{2,1,0:T(1,128)S(1)} async-done(((f32[8,1,128]{2,1,0:T(1,128)}), f32[8,1,128]{2,1,0:T(1,128)S(1)}, u32[]{:S(2)}, u32[]{:S(2)}) %all-to-all-start) | async-done | bytes 4128 | tf_op jit(solution)/shard_map/all_to_all | solution.py:16
  20.5 2.0 fusion.2
  22.6 107.4 %all-gather.3.cloned.1.call-done = bf16[4096,2048]{1,0:T(8,128)(2,1)} async-done(((bf16[128,2048]{1,0:T(8,128)(2,1)}), bf16[4096,2048]{1,0:T(8,128)(2,1)}) %all-gather.3.cloned.1.call-update) | async-done | bytes 16777232 | tf_op jit(solution)/shard_map/all_gather | solution.py:66
  130.0 10.9 %convolution_convert_fusion.1 = bf16[4096,64]{0,1:T(8,128)(2,1)S(1)} fusion(bf16[4096,2048]{1,0:T(8,128)(2,1)} %all-gather.3.cloned.1.call-done, bf16[2048,64]{0,1:T(8,128)(2,1)} %param.9), kind=kOutput, calls=%fused_computation.2 | convolution fusion | flops 1074003968 | bytes 17563648 | tf_op jit(solution)/shard_map/dot_general | solution.py:71
  140.9 0.8 copy.51
  141.8 18.8 %all-to-all-start.2 = ((bf16[8,512,64]{1,2,0:T(8,128)(2,1)}), bf16[8,512,64]{1,2,0:T(8,128)(2,1)S(1)}, u32[]{:S(2)}, u32[]{:S(2)}) async-start(bf16[8,512,64]{1,2,0:T(8,128)(2,1)} %bitcast.22), calls=%async_computation.2 | async-start | bytes 1048576 | tf_op jit(solution)/shard_map/all_to_all | solution.py:31
  160.6 13.7 %convolution_convert_fusion = bf16[4096,512]{1,0:T(8,128)(2,1)} fusion(bf16[4096,2048]{1,0:T(8,128)(2,1)} %all-gather.3.cloned.1.call-done, bf16[2048,512]{1,0:T(8,128)(2,1)S(1)} %copy-done), kind=kOutput, calls=%fused_computation.1 | convolution fusion | flops 8592031744 | bytes 23068672 | tf_op jit(solution)/shard_map/dot_general | solution.py:68
  174.4 5.3 %all-to-all-start.1 = ((bf16[8,512,512]{2,1,0:T(8,128)(2,1)}), bf16[8,512,512]{2,1,0:T(8,128)(2,1)}, u32[]{:S(2)}, u32[]{:S(2)}) async-start(bf16[8,512,512]{2,1,0:T(8,128)(2,1)} %bitcast.23), calls=%async_computation.1 | async-start | bytes 8388608 | tf_op jit(solution)/shard_map/all_to_all | solution.py:31
  179.6 0.2 all-gather.5.cloned.1.call-start
  180.0 0.1 broadcast_in_dim.26
  180.3 0.1 fusion.25
  180.4 0.3 fusion.15
  180.9 0.7 select_convert_fusion
  181.6 0.1 dynamic_slice.3
  181.7 57.3 %all-gather.5.cloned.1.call-done = bf16[512,2048]{0,1:T(8,128)(2,1)} async-done(((bf16[512,64]{0,1:T(8,128)(2,1)}), bf16[512,2048]{0,1:T(8,128)(2,1)}) %all-gather.5.cloned.1.call-update) | async-done | bytes 2097168 | tf_op jit(solution)/shard_map/all_gather | solution.py:82
  239.0 4.6 %copy.40 = bf16[512,8,256]{2,1,0:T(8,128)(2,1)} copy(bf16[512,8,256]{0,2,1:T(8,128)(2,1)} %bitcast.25) | data formatting | bytes 4194304 | tf_op jit(solution)/shard_map/reshape | solution.py:85
  243.6 2.3 convolution_convert_fusion.2
  245.9 0.9 copy.39
  246.8 2.9 %convert_reduce_fusion = f32[512,512]{1,0:T(8,128)S(1)} fusion(bf16[8,512,512]{2,1,0:T(8,128)(2,1)} %all-to-all-done.1), kind=kLoop, calls=%fused_computation | loop fusion | flops 3932160 | bytes 5242880 | tf_op jit(solution)/shard_map/reduce_sum | solution.py:32
  249.7 1.3 copy.29
  251.0 1.8 reshape.312
  252.8 1.8 fusion.24
  254.6 1.2 copy.41
  255.9 1.2 copy.42
  257.1 2.4 fusion.8
  259.5 0.5 copy.32
  260.1 0.2 convert_element_type.58
  260.3 1.0 copy.38
  (24 shorter events, 0.6 us)
Async XLA Ops:
  7.2 153.5 %copy-start = (bf16[2048,512]{1,0:T(8,128)(2,1)S(1)}, bf16[2048,512]{1,0:T(8,128)(2,1)}, u32[]{:S(2)}) copy-start(bf16[2048,512]{1,0:T(8,128)(2,1)} %param.8) | copy-start | bytes 6291460
  9.2 11.3 %all-to-all-start = ((f32[8,1,128]{2,1,0:T(1,128)}), f32[8,1,128]{2,1,0:T(1,128)S(1)}, u32[]{:S(2)}, u32[]{:S(2)}) async-start(f32[8,1,128]{2,1,0:T(1,128)} %broadcast_in_dim.14), calls=%async_computation | async-start | bytes 8192 | tf_op jit(solution)/shard_map/all_to_all | solution.py:16
  15.5 114.5 %all-gather.3.cloned.1.call-start = ((), (), s32[]{:S(2)}) async-start(), calls=%async_computation.3 | async-start | bytes 17301504 | tf_op jit(solution)/shard_map/all_gather | solution.py:66
  141.8 32.6 %all-to-all-start.2 = ((bf16[8,512,64]{1,2,0:T(8,128)(2,1)}), bf16[8,512,64]{1,2,0:T(8,128)(2,1)S(1)}, u32[]{:S(2)}, u32[]{:S(2)}) async-start(bf16[8,512,64]{1,2,0:T(8,128)(2,1)} %bitcast.22), calls=%async_computation.2 | async-start | bytes 1048576 | tf_op jit(solution)/shard_map/all_to_all | solution.py:31
  174.4 5.5 %copy-start.1 = (s32[512]{0:T(512)S(1)}, s32[512]{0:T(512)}, u32[]{:S(2)}) copy-start(s32[512]{0:T(512)} %param.10) | copy-start | bytes 6148
  174.4 7.3 %copy-start.2 = (s32[8]{0:T(128)S(1)}, s32[8]{0:T(128)}, u32[]{:S(2)}) copy-start(s32[8]{0:T(128)} %param.11) | copy-start | bytes 100
  174.4 72.4 %all-to-all-start.1 = ((bf16[8,512,512]{2,1,0:T(8,128)(2,1)}), bf16[8,512,512]{2,1,0:T(8,128)(2,1)}, u32[]{:S(2)}, u32[]{:S(2)}) async-start(bf16[8,512,512]{2,1,0:T(8,128)(2,1)} %bitcast.23), calls=%async_computation.1 | async-start | bytes 8388608 | tf_op jit(solution)/shard_map/all_to_all | solution.py:31
  179.6 59.4 %all-gather.5.cloned.1.call-start = ((), (), s32[]{:S(2)}) async-start(), calls=%async_computation.4 | async-start | bytes 2162688 | tf_op jit(solution)/shard_map/all_gather | solution.py:82
Sparse Core Ops, SparseCore 0:
  22.7 107.2 all-gather.2
  183.6 55.3 all-gather.4
where the time goes:
time: 269 us; the launch traced here: 268 us
  waiting for transfers between devices  169 us (63%)
  starting transfers between devices  30.7 us (11%)
  matrix products  27 us (10%)
  local copies, waits for them, and re-layouts  16.5 us (6%)
  between operations  14.2 us (5%)
  other arithmetic  10.6 us (4%)
    all_gather x1, waiting for transfers between devices, body(): gathered = lax.all_gather(normed_rows, ('gx', 'gy'), axis=0, tiled=True)  107 us
    all_gather x1, waiting for transfers between devices, body(): keyval_all = lax.all_gather(keyval_part, ('gx', 'gy'), axis=1, tiled=True)  57.3 us
    all_to_all x2, starting transfers between devices, summed_on_arrival(): lax.all_to_all(in_blocks(value, dim, count), axis, 0, 0, tiled=True)  24.1 us
    dot_general x1, matrix products, body(): jnp.dot(gathered, w_query, preferred_element_type=jnp.float32)  13.7 us
    dot_general x1, matrix products, body(): jnp.dot(gathered, w_keyval, preferred_element_type=jnp.float32)  10.9 us
    all_to_all x1, starting transfers between devices, from_everyone(): return lax.all_to_all(copies, axis, split_axis=0, concat_axis=0, tiled=True)  6.36 us
  transfers between devices with their start and end apart: 5, of which 3 were waited for; matrix products, arithmetic and copies ran while one was open for 9% of the time, Pallas kernels for 0%

commit v1 on v0

--- a/solution.py
+++ b/solution.py
@@ -9,6 +9,13 @@
 HD = 128
 rope_base = 500000.0
 norm_eps = 1e-05
+
+
+def pack_files(unit):
+    return jnp.concatenate(
+        lax.all_to_all(jnp.stack(lax.axis_size(("gx", "gy")) * [unit], axis=0), ("gx", "gy"), 0, 0),
+        axis=0,
+    )
 
 
 def from_everyone(value, axis):
@@ -63,7 +70,7 @@
     query_width = w_query.shape[1]
     keyval_width = w_keyval.shape[1]
     group_size = lax.axis_size("gy")
-    gathered = lax.all_gather(normed_rows, ("gx", "gy"), axis=0, tiled=True)
+    gathered = pack_files(normed_rows)
     query_sum = summed_on_arrival(
         jnp.dot(gathered, w_query, preferred_element_type=jnp.float32).astype(jnp.bfloat16), "gz", 0
     )

time: 269 us -> 526 us (1.96)
  blocking collectives: 0 us -> 378 us
  waiting for transfers between devices: 169 us -> 63.3 us
  starting transfers between devices: 30.7 us -> 15.3 us
  local copies, waits for them, and re-layouts: 16.5 us -> 23.1 us
  matrix products: 27 us -> 21.3 us
    all_to_all x0 -> x1, blocking collectives: none -> 378 us  [pack_files(): lax.all_to_all(jnp.stack(lax.axis_size(('gx', 'gy')) * [unit], axis=0), (...]
    all_gather x1 -> x0, waiting for transfers between devices: 107 us -> none  [body(): gathered = lax.all_gather(normed_rows, ('gx', 'gy'), axis=0, tiled=True)]
    all_to_all x2, starting transfers between devices: 24.1 us -> 8.7 us  [summed_on_arrival(): lax.all_to_all(in_blocks(value, dim, count), axis, 0, 0, tiled=True)]
    another operation x0 -> x1, local copies, waits for them, and re-layouts: none -> 5.99 us  [pack_files(): jnp.stack(lax.axis_size(('gx', 'gy')) * [unit], axis=0)]
    dot_general x1, matrix products: 10.9 us -> 5.17 us  [body(): jnp.dot(gathered, w_keyval, preferred_element_type=jnp.float32)]
  transfers between devices with their start and end apart: 5 -> 4, of which waited for: 3 -> 2; matrix products, arithmetic and copies ran while one was open for 9% -> 5% of each run, Pallas kernels for 0% -> 0%
where the time goes in v1:
time: 526 us; the launch traced here: 525 us
  blocking collectives  378 us (72%)
  waiting for transfers between devices  63.3 us (12%)
  local copies, waits for them, and re-layouts  23.1 us (4%)
  matrix products  21.3 us (4%)
  starting transfers between devices  15.3 us (3%)
  between operations  14.2 us (3%)
  other arithmetic  9.8 us (2%)
    all_to_all x1, blocking collectives, pack_files(): lax.all_to_all(jnp.stack(lax.axis_size(('gx', 'gy')) * [unit], axis=0), (...  378 us
    all_gather x1, waiting for transfers between devices, body(): keyval_all = lax.all_gather(keyval_part, ('gx', 'gy'), axis=1, tiled=True)  59 us
    dot_general x1, matrix products, body(): jnp.dot(gathered, w_query, preferred_element_type=jnp.float32)  13.7 us
  transfers between devices with their start and end apart: 4, of which 2 were waited for; matrix products, arithmetic and copies ran while one was open for 5% of the time, Pallas kernels for 0%

profile of v1, /device:TPU:1, one launch (start us, length us, event | category | flops | bytes accessed | tf_op | source)
XLA Modules:
  0.0 525.3 jit_solution(15483415424193471161)
XLA Ops:
  7.2 1.4 fusion
  8.6 0.6 broadcast_in_dim.14
  9.2 6.4 %all-to-all-start = ((f32[8,1,128]{2,1,0:T(1,128)}), f32[8,1,128]{2,1,0:T(1,128)S(1)}, u32[]{:S(2)}, u32[]{:S(2)}) async-start(f32[8,1,128]{2,1,0:T(1,128)} %broadcast_in_dim.14), calls=%async_computation | async-start | bytes 8192 | tf_op jit(solution)/shard_map/all_to_all | solution.py:23
  15.5 0.7 convert_element_type.52
  16.2 4.3 all-to-all-done
  20.5 1.2 fusion.2
  21.7 6.0 %stack.9 = bf16[32,128,2048]{2,1,0:T(8,128)(2,1)} broadcast(bf16[128,2048]{1,0:T(8,128)(2,1)S(1)} %fusion.2), dimensions={1,2} | broadcast | bytes 17301504 | tf_op jit(solution)/shard_map/stack | solution.py:16
  27.7 378.3 %all_to_all.21 = bf16[32,128,2048]{2,1,0:T(8,128)(2,1)S(1)} all-to-all(bf16[32,128,2048]{2,1,0:T(8,128)(2,1)} %stack.9), channel_id=1, replica_groups=mesh['gx'=8,'gy'=4,'gz'=8] {'gx','gy'}, dimensions={0} | all-to-all | bytes 33554432 | tf_op jit(solution)/shard_map/all_to_all | solution.py:16
  406.0 5.2 convolution_convert_fusion.1
  411.2 0.6 copy-done.1
  411.8 0.8 copy.51
  412.6 3.5 all-to-all-start.3
  416.1 13.7 %convolution_convert_fusion = bf16[4096,512]{1,0:T(8,128)(2,1)} fusion(bf16[4096,2048]{1,0:T(8,128)(2,1)} %bitcast.25, bf16[2048,512]{1,0:T(8,128)(2,1)S(1)} %copy-done), kind=kOutput, calls=%fused_computation.1 | convolution fusion | flops 8592031744 | bytes 23068672 | tf_op jit(solution)/shard_map/dot_general | solution.py:75
  429.9 5.2 all-to-all-start.2
  435.1 0.2 all-gather.2.cloned.1.call-start
  435.4 0.1 broadcast_in_dim.26
  435.8 0.3 fusion.15
  436.3 0.7 select_convert_fusion
  437.2 59.0 %all-gather.2.cloned.1.call-done = bf16[512,2048]{0,1:T(8,128)(2,1)} async-done(((bf16[512,64]{0,1:T(8,128)(2,1)}), bf16[512,2048]{0,1:T(8,128)(2,1)}) %all-gather.2.cloned.1.call-update) | async-done | bytes 2097168 | tf_op jit(solution)/shard_map/all_gather | solution.py:89
  496.2 4.6 copy.40
  500.7 2.3 convolution_convert_fusion.2
  503.1 0.9 copy.39
  503.9 2.9 convert_reduce_fusion
  506.8 1.3 copy.29
  508.1 1.8 reshape.318
  510.0 1.8 fusion.24
  511.8 1.2 copy.42
  513.0 1.2 copy.41
  514.3 2.4 fusion.8
  516.7 0.5 copy.32
  517.2 0.2 convert_element_type.58
  517.4 1.0 copy.38
  (27 shorter events, 0.7 us)
Async XLA Ops:
  7.2 408.9 %copy-start = (bf16[2048,512]{1,0:T(8,128)(2,1)S(1)}, bf16[2048,512]{1,0:T(8,128)(2,1)}, u32[]{:S(2)}) copy-start(bf16[2048,512]{1,0:T(8,128)(2,1)} %param.8) | copy-start | bytes 6291460
  9.2 11.3 %all-to-all-start = ((f32[8,1,128]{2,1,0:T(1,128)}), f32[8,1,128]{2,1,0:T(1,128)S(1)}, u32[]{:S(2)}, u32[]{:S(2)}) async-start(f32[8,1,128]{2,1,0:T(1,128)} %broadcast_in_dim.14), calls=%async_computation | async-start | bytes 8192 | tf_op jit(solution)/shard_map/all_to_all | solution.py:23
  27.7 378.3 %copy-start.2 = (bf16[2048,64]{0,1:T(8,128)(2,1)S(1)}, bf16[2048,64]{0,1:T(8,128)(2,1)}, u32[]{:S(2)}) copy-start(bf16[2048,64]{0,1:T(8,128)(2,1)} %param.9) | copy-start | bytes 786436
  406.0 5.7 %copy-start.1 = (bf16[32,128,2048]{2,1,0:T(8,128)(2,1)}, bf16[32,128,2048]{2,1,0:T(8,128)(2,1)S(1)}, u32[]{:S(2)}) copy-start(bf16[32,128,2048]{2,1,0:T(8,128)(2,1)S(1)} %all_to_all.21) | copy-start | bytes 50331652
  412.6 17.3 %all-to-all-start.3 = ((bf16[8,512,64]{1,2,0:T(8,128)(2,1)}), bf16[8,512,64]{1,2,0:T(8,128)(2,1)S(1)}, u32[]{:S(2)}, u32[]{:S(2)}) async-start(bf16[8,512,64]{1,2,0:T(8,128)(2,1)} %bitcast.23), calls=%async_computation.3 | async-start | bytes 1048576 | tf_op jit(solution)/shard_map/all_to_all | solution.py:38
  429.9 5.4 %copy-start.3 = (s32[512]{0:T(512)S(1)}, s32[512]{0:T(512)}, u32[]{:S(2)}) copy-start(s32[512]{0:T(512)} %param.10) | copy-start | bytes 6148
  429.9 7.2 %copy-start.4 = (s32[8]{0:T(128)S(1)}, s32[8]{0:T(128)}, u32[]{:S(2)}) copy-start(s32[8]{0:T(128)} %param.11) | copy-start | bytes 100
  429.9 74.1 %all-to-all-start.2 = ((bf16[8,512,512]{2,1,0:T(8,128)(2,1)}), bf16[8,512,512]{2,1,0:T(8,128)(2,1)}, u32[]{:S(2)}, u32[]{:S(2)}) async-start(bf16[8,512,512]{2,1,0:T(8,128)(2,1)} %bitcast.26), calls=%async_computation.2 | async-start | bytes 8388608 | tf_op jit(solution)/shard_map/all_to_all | solution.py:38
  435.1 61.1 %all-gather.2.cloned.1.call-start = ((), (), s32[]{:S(2)}) async-start(), calls=%async_computation.4 | async-start | bytes 2162688 | tf_op jit(solution)/shard_map/all_gather | solution.py:89
Sparse Core Ops, SparseCore 0:
  439.0 57.0 all-gather.1
